TPU v7x, 8 devices: a whole 2x2x1 slice. The times are simulated.
8 devices in a mesh: dp: 2 (over z, y), tp: 4 (over x, core).
Axes of the slice: x: 2, y: 2, z: 1, core: 2. Of those that a mesh axis runs over, the one named last changes fastest.
Arguments:
- x_in: bfloat16 [8, 1024, 640], P('dp', 'tp'), parts along dimension 0
- grad_y: bfloat16 [8, 1024, 640], P('dp', 'tp'), parts along dimension 0
- pad_mask: int32 [8, 1024], P('dp'), parts along dimension 0
- ln1_gain: float32 [640], replicated
- ln1_bias: float32 [640], replicated
- w_qkv: bfloat16 [3, 640, 20, 32], P(None, None, 'tp')
- b_qkv: float32 [3, 20, 32], P(None, 'tp')
- w_out: bfloat16 [20, 32, 640], P('tp')
- b_out: float32 [640], replicated
- ln2_gain: float32 [640], replicated
- ln2_bias: float32 [640], replicated
- w_up: bfloat16 [640, 2560], P(None, 'tp')
- b_up: float32 [2560], P('tp')
- w_down: bfloat16 [2560, 640], P('tp')
- b_down: float32 [640], replicated
Outputs:
- output 1: bfloat16 [8, 1024, 640], P('dp', 'tp'), parts along dimension 0
- output 2: bfloat16 [8, 1024, 640], P('dp', 'tp'), parts along dimension 0
- output 3: float32 [1280], P('dp'), parts along dimension 0
- output 4: float32 [1280], P('dp'), parts along dimension 0
- output 5: float32 [6, 640, 20, 32], P('dp', None, 'tp'), parts along dimension 0
- output 6: float32 [6, 20, 32], P('dp', 'tp'), parts along dimension 0
- output 7: float32 [40, 32, 640], P(('dp', 'tp')), parts along dimension 0
- output 8: float32 [1280], P('dp'), parts along dimension 0
- output 9: float32 [1280], P('dp'), parts along dimension 0
- output 10: float32 [1280], P('dp'), parts along dimension 0
- output 11: float32 [1280, 2560], P('dp', 'tp'), parts along dimension 0
- output 12: float32 [5120], P(('dp', 'tp')), parts along dimension 0
- output 13: float32 [5120, 640], P(('dp', 'tp')), parts along dimension 0
- output 14: float32 [1280], P('dp'), parts along dimension 0
There are 2 independent parts. A program takes and returns all parts, laid end to end along the dimension named above; an argument that names none is the same for every part.
All inputs are finite; a program needn't handle non-finite values.
Results may differ from a plain program's by a relative error of at most 0.0125188.
Values are sent between devices in bfloat16 or wider.
A program may use at most 1 GiB of HBM per device.

v0:
```python
import functools

import jax
import jax.numpy as jnp
from jax import lax
from jax.experimental import pallas as pl
from jax.experimental.pallas import tpu as pltpu
from jax.sharding import PartitionSpec as P

LN_EPS = 1e-5
ROPE_BASE = 10000.0
INV_SQRT2 = 0.7071067811865476
INV_SQRT_2PI = 0.3989422804014327
NEG_LARGE = -1e30
F32 = jnp.float32
BF16 = jnp.bfloat16
MESH = pl.DeviceIdType.MESH


def dot(lhs, rhs):
    return jnp.dot(lhs, rhs, preferred_element_type=F32)


def layer_norm(values, ln_gain, ln_bias):
    centered = values - jnp.mean(values, axis=-1, keepdims=True)
    inv_std = lax.rsqrt(jnp.mean(centered * centered, axis=-1, keepdims=True) + LN_EPS)
    x_hat = centered * inv_std
    return x_hat * ln_gain + ln_bias, x_hat, inv_std


def rope_tables(seq_len, head_dim):
    half_dim = head_dim // 2
    inv_freq = ROPE_BASE ** (-2.0 * jnp.arange(half_dim, dtype=F32) / head_dim)
    angles = inv_freq[:, None] * jnp.arange(seq_len, dtype=F32)[None, :]
    angles = jnp.concatenate([angles, angles], axis=0)
    return jnp.cos(angles), jnp.sin(angles)


def remote(src, dst, send_sem, recv_sem, device):
    return pltpu.make_async_remote_copy(src_ref=src, dst_ref=dst, send_sem=send_sem, recv_sem=recv_sem, device_id={'tp': device}, device_id_type=MESH)


def greet(me):
    barrier = pltpu.get_barrier_semaphore()
    for mask in (1, 2, 3):
        pl.semaphore_signal(barrier, inc=1, device_id={'tp': me ^ mask}, device_id_type=MESH)
    pl.semaphore_wait(barrier, 3)


class Gather:
    def __init__(self, src, dst, base, send_sem, recv_sem, me):
        self.near = remote(src, dst.at[1 - base], send_sem.at[0], recv_sem.at[0], me ^ 1)
        self.far = remote(src, dst.at[2 - base], send_sem.at[1], recv_sem.at[1], me ^ 2)
        self.relay = remote(dst.at[2 - base], dst.at[3 - base], send_sem.at[2], recv_sem.at[2], me ^ 1)

    def start(self):
        self.far.start()
        self.near.start()

    def forward(self):
        self.far.wait_recv()
        self.relay.start()

    def finish(self):
        self.near.wait()
        self.far.wait_send()
        self.relay.wait()


class ToSequence:
    def __init__(self, src, dst, send_sem, recv_sem, me, chunk):
        self.copies = {mask: remote(src.at[me ^ mask], dst.at[pl.ds(pl.multiple_of(me * chunk, chunk), chunk)], send_sem.at[mask], recv_sem.at[mask], me ^ mask) for mask in (2, 3, 1)}

    def start(self):
        for copy in self.copies.values():
            copy.start()

    def wait_recv(self):
        for copy in self.copies.values():
            copy.wait_recv()

    def wait_send(self):
        for copy in self.copies.values():
            copy.wait_send()


def forward_kernel(dims, x_ref, wq_ref, bq_ref, mask_ref, gain_ref, bias_ref, cos_ref, sin_ref, wo_ref, wu_ref, wd_ref, bu_ref, dy_ref,
                   x_full, wq_all, h1_ref, q_all, k_all, v_all, o_ref, wide_ref, lse_ref, wo_all, wu_all, wd_all, bu_all, dy_full,
                   h1t_ref, bq_all, own_sem, send_sem, recv_sem):
    chunk, local_heads, head_dim = dims
    me = lax.axis_index('tp')
    half = head_dim // 2
    greet(me)
    x_move = ToSequence(x_ref, x_full, send_sem.at[0], recv_sem.at[0], me, chunk)
    dy_move = ToSequence(dy_ref, dy_full, send_sem.at[1], recv_sem.at[1], me, chunk)
    wq = Gather(wq_ref, wq_all, 0, send_sem.at[2], recv_sem.at[2], me)
    bq = Gather(bq_ref, bq_all, 0, send_sem.at[3], recv_sem.at[3], me)
    others = [Gather(src, dst, 1, send_sem.at[4 + i], recv_sem.at[4 + i], me) for i, (src, dst) in enumerate(((wo_ref, wo_all), (bu_ref, bu_all), (wu_ref, wu_all), (wd_ref, wd_all)))]
    x_move.start()
    bq.start()
    wq.start()
    own_wq = pltpu.make_async_copy(wq_ref, wq_all.at[0], own_sem.at[0])
    own_wq.start()
    own_rows = pl.ds(pl.multiple_of(me * chunk, chunk), chunk)
    own_dy = pltpu.make_async_copy(dy_ref.at[me], dy_full.at[own_rows], own_sem.at[1])
    own_dy.start()
    for move in others[:3]:
        move.start()
    dy_move.start()
    others[3].start()
    x_full[own_rows] = x_ref[me]
    bq_all[0] = bq_ref[...]
    x_move.wait_recv()
    x_f = x_full[...].astype(F32)
    h1, _, _ = layer_norm(x_f, gain_ref[...], bias_ref[...])
    h1 = h1.astype(BF16)
    h1_ref[...] = h1
    h1t_ref[...] = h1.T
    own_wq.wait()

    @pl.loop(0, 4)
    def _(m):
        @pl.when(m == 1)
        def _():
            bq.near.wait_recv()
            wq.near.wait_recv()

        @pl.when(m == 2)
        def _():
            bq.forward()
            wq.forward()

        @pl.when(m == 3)
        def _():
            bq.relay.wait_recv()
            wq.relay.wait_recv()

        bias = bq_all[m].T[:, :1]
        qkv = dot(wq_all[m], h1t_ref[...]) + bias
        cos, sin = cos_ref[...], sin_ref[...]
        group = local_heads * head_dim
        ones = (lax.broadcasted_iota(jnp.int32, (half, cos.shape[1]), 0) == 0).astype(BF16)
        for j in range(local_heads):
            head = m * local_heads + j
            for which, (dst, scale, extra) in enumerate(((q_all, head_dim ** -0.5, ones), (k_all, None, mask_ref[...]))):
                rows = qkv[which * group + j * head_dim:which * group + (j + 1) * head_dim]
                rows = rows * scale if scale is not None else rows
                low, high = rows[:half], rows[half:]
                dst[head, :half] = (low * cos - high * sin).astype(BF16)
                dst[head, half:head_dim] = (high * cos + low * sin).astype(BF16)
                dst[head, head_dim:] = extra
            v_all[head] = qkv[2 * group + j * head_dim:2 * group + (j + 1) * head_dim].astype(BF16)

        @pl.loop(0, local_heads)
        def _(j):
            head = m * local_heads + j
            scores = dot(k_all[head].T, q_all[head])
            top = jnp.max(scores, axis=0, keepdims=True)
            weights = jnp.exp(scores - top)
            total = jnp.sum(weights, axis=0, keepdims=True)
            out = dot(v_all[head], weights.astype(BF16)) / total
            o_ref[head] = out.astype(BF16)
            wide_ref[head] = out
            lse_ref[head] = top + jnp.log(total)

    x_move.wait_send()
    for move in (bq, wq):
        move.near.wait_send()
        move.far.wait_send()
        move.relay.wait_send()
    for move in others:
        move.forward()
    for move in others:
        move.finish()
    own_dy.wait()
    dy_move.wait_recv()
    dy_move.wait_send()


def forward_call(x_in, wq, bq, key_bias, gain, bias, cos, sin, wo, wu, wd, bu, dy, local_heads, head_dim):
    tp, chunk, width = x_in.shape
    seq_len = tp * chunk
    heads = tp * local_heads
    ext = head_dim + head_dim // 2
    vmem, anywhere = pl.BlockSpec(memory_space=pltpu.VMEM), pl.BlockSpec(memory_space=pl.ANY)

    def shape(dims, dtype=BF16):
        return jax.ShapeDtypeStruct(dims, dtype)

    outs = [shape((seq_len, width)), shape((tp,) + wq.shape), shape((seq_len, width)), shape((heads, ext, seq_len)), shape((heads, ext, seq_len)),
            shape((heads, head_dim, seq_len)), shape((heads, head_dim, seq_len)), shape((heads, head_dim, seq_len), F32), shape((heads, 1, seq_len), F32),
            shape((tp - 1,) + wo.shape), shape((tp - 1,) + wu.shape), shape((tp - 1,) + wd.shape), shape((tp - 1,) + bu.shape, F32), shape((seq_len, width))]
    return pl.pallas_call(
        functools.partial(forward_kernel, (chunk, local_heads, head_dim)),
        out_shape=outs,
        in_specs=[vmem, anywhere] + [vmem] * 6 + [anywhere] * 5,
        out_specs=[vmem] * 9 + [anywhere] * 5,
        scratch_shapes=[pltpu.VMEM((width, seq_len), BF16), pltpu.VMEM((tp,) + bq.shape, F32), pltpu.SemaphoreType.DMA((2,)), pltpu.SemaphoreType.DMA((8, 4)), pltpu.SemaphoreType.DMA((8, 4))],
        compiler_params=pltpu.CompilerParams(collective_id=0, has_side_effects=True, vmem_limit_bytes=60 << 20),
        name='forward',
    )(x_in, wq, bq, key_bias, gain, bias, cos, sin, wo, wu, wd, bu, dy)


def layer_norm_rows(values, ln_gain, ln_bias):
    centered = values - jnp.mean(values, axis=0, keepdims=True)
    inv_std = lax.rsqrt(jnp.mean(centered * centered, axis=0, keepdims=True) + LN_EPS)
    x_hat = centered * inv_std
    return x_hat * ln_gain + ln_bias, x_hat, inv_std


def layer_norm_rows_grad(d_out, x_hat, inv_std, ln_gain):
    d_hat = d_out * ln_gain
    return inv_std * (d_hat - jnp.mean(d_hat, axis=0, keepdims=True) - x_hat * jnp.mean(d_hat * x_hat, axis=0, keepdims=True))


def dot_tn(lhs, rhs):
    return lax.dot_general(lhs, rhs, (((0,), (0,)), ((), ())), preferred_element_type=F32)


def dot_nt(lhs, rhs):
    return lax.dot_general(lhs, rhs, (((1,), (1,)), ((), ())), preferred_element_type=F32)


def gelu(pre_act):
    half_erf = 0.5 * (1.0 + lax.erf(pre_act * INV_SQRT2))
    act = (pre_act * half_erf).astype(BF16)
    return act, half_erf + pre_act * jnp.exp(-0.5 * pre_act * pre_act) * INV_SQRT_2PI


class FromSequence:
    def __init__(self, src, dst, send_sem, recv_sem, me, chunk):
        self.copies = {mask: remote(src.at[pl.ds(pl.multiple_of((me ^ mask) * chunk, chunk), chunk)], dst.at[me], send_sem.at[mask], recv_sem.at[mask], me ^ mask) for mask in (2, 3, 1)}

    def start(self):
        for copy in self.copies.values():
            copy.start()

    def wait(self):
        for copy in self.copies.values():
            copy.wait()


def middle_kernel(x_ref, o_ref, wo_ref, wo_far_ref, vec_ref, bu_ref, dy_ref, wu_own, wu_far, wd_own, wd_far,
                  y_ref, h2_ref, dx1t_ref, dx1b_ref, do_ref, sums_ref,
                  wu_all, wd_all, slope_ref, act_ref, y_seq, load_sem, send_sem, recv_sem):
    me = lax.axis_index('tp')
    tp, chunk, width = y_ref.shape
    ff = wu_own.shape[1]
    greet(me)
    loads = []
    for m in range(tp):
        wu_src = wu_own if m == 0 else wu_far.at[m - 1]
        wd_src = wd_own if m == 0 else wd_far.at[m - 1]
        loads.append((pltpu.make_async_copy(wu_src, wu_all.at[m], load_sem.at[0, m]), pltpu.make_async_copy(wd_src, wd_all.at[m], load_sem.at[1, m])))
    for load, _ in loads:
        load.start()
    for _, load in loads:
        load.start()
    cols = vec_ref[...].T
    b_out, gain, bias, b_down = (cols[:, i:i + 1] for i in range(4))
    rows = wo_ref.shape[0]
    attn = dot_tn(wo_ref[...], o_ref[:rows]) + dot_tn(wo_far_ref[...], o_ref[rows:])
    x1 = (x_ref[...].T.astype(F32) + (attn + b_out)).astype(BF16).astype(F32)
    h2_f, x_hat, inv_std = layer_norm_rows(x1, gain, bias)
    h2 = h2_f.astype(BF16)
    h2_ref[...] = h2.T
    for load, _ in loads:
        load.wait()

    @pl.loop(0, tp)
    def _(m):
        pre_act = dot_tn(wu_all[m], h2) + bu_ref[m].T[:, :1]
        act, slope = gelu(pre_act)
        act_ref[m] = act
        slope_ref[m] = slope

    for _, load in loads:
        load.wait()
    mlp = dot_tn(wd_all[...].reshape(tp * ff, width), act_ref[...].reshape(tp * ff, tp * chunk))
    y_seq[...] = (x1 + (mlp + b_down)).astype(BF16).T
    dy = dy_ref[...]
    dy_t = dy.T
    dy_f = dy_t.astype(F32)

    @pl.loop(0, tp)
    def _(m):
        act_ref[m] = (dot(wd_all[m], dy_t) * slope_ref[m]).astype(BF16)

    y_move = FromSequence(y_seq, y_ref, send_sem, recv_sem, me, chunk)
    y_move.start()
    y_ref[me] = y_seq[pl.ds(pl.multiple_of(me * chunk, chunk), chunk)]
    d_h2 = dot(wu_all[0], act_ref[0])
    for m in range(1, tp):
        d_h2 = d_h2 + dot(wu_all[m], act_ref[m])
    d_x1 = dy_f + layer_norm_rows_grad(d_h2, x_hat, inv_std, gain)
    dx1t_ref[...] = d_x1
    d_x1_b = d_x1.astype(BF16)
    dx1b_ref[...] = d_x1_b.T
    do_ref[:rows] = dot(wo_ref[...], d_x1_b).astype(BF16)
    do_ref[rows:] = dot(wo_far_ref[...], d_x1_b).astype(BF16)

    def lane_sum(value):
        return jnp.sum(value, axis=1, keepdims=True)

    sums = [lane_sum(dy_f), lane_sum(d_h2 * x_hat), lane_sum(d_h2), lane_sum(d_x1)]
    sums_ref[...] = jnp.concatenate(sums + [jnp.zeros((width, 124), F32)], axis=1).T[:8]
    y_move.wait()


def backward_kernel(dims, q_all, k_all, v_all, do_ref, wide_ref, lse_ref, cos_ref, sin_ref, o_ref, dx1b_ref, h2_ref, dy_ref,
                    dqkv_ref, gb_ref, gwo_ref, h2_all, dy_all,
                    part, near_buf, far_buf, red_send, red_recv, send_sem, recv_sem):
    local_heads, head_dim = dims
    me = lax.axis_index('tp')
    tp = part.shape[0]
    half = head_dim // 2
    greet(me)
    h2_move = Gather(h2_ref, h2_all, 1, send_sem.at[0], recv_sem.at[0], me)
    dy_move = Gather(dy_ref, dy_all, 1, send_sem.at[1], recv_sem.at[1], me)
    h2_move.start()
    dy_move.start()
    reduce_near = [remote(part.at[src], near_buf.at[i], red_send.at[i], red_recv.at[i], me ^ 1) for i, src in enumerate((1, 3))]
    reduce_far = remote(part.at[2], far_buf, red_send.at[2], red_recv.at[2], me ^ 2)
    part[...] = dot(o_ref[...], dx1b_ref[...]).reshape(part.shape)
    cos, sin = cos_ref[...], sin_ref[...]

    def store(m, j, which, low, high):
        grad = jnp.concatenate([low, high], axis=0)
        dqkv_ref[m, which, pl.ds(pl.multiple_of(j * head_dim, head_dim), head_dim)] = grad.astype(BF16)
        gb_ref[m, which, pl.ds(pl.multiple_of(j * head_dim, head_dim), head_dim)] = jnp.broadcast_to(jnp.sum(grad, axis=1, keepdims=True), (head_dim, 128))

    def back(grad):
        low, high = grad[:half], grad[half:]
        return low * cos + high * sin, high * cos - low * sin

    @pl.loop(0, tp * local_heads)
    def _(head):
        m = lax.div(head, local_heads)
        j = lax.rem(head, local_heads)

        @pl.when(head == 1)
        def _():
            for copy in reduce_near:
                copy.start()

        @pl.when(head == 4)
        def _():
            for copy in reduce_near:
                copy.wait()
            part[0] += near_buf[0]
            part[2] += near_buf[1]

        @pl.when(head == 5)
        def _():
            reduce_far.start()

        @pl.when(head == 12)
        def _():
            h2_move.forward()

        q, k, v, d_out = q_all[head], k_all[head], v_all[head], do_ref[head]
        delta = jnp.sum(d_out.astype(F32) * wide_ref[head], axis=0, keepdims=True)
        probs = jnp.exp(dot(k.T, q) - lse_ref[head])
        d_probs = dot(v.T, d_out)
        d_scores = (probs * (d_probs - delta)).astype(BF16)
        d_value = dot(probs.astype(BF16), d_out.T).T
        d_key = dot(d_scores, q[:head_dim].T).T
        d_query = dot(k[:head_dim], d_scores)
        low, high = back(d_query)
        scale = head_dim ** -0.5
        store(m, j, 0, low * scale, high * scale)
        low, high = back(d_key)
        store(m, j, 1, low, high)
        store(m, j, 2, d_value[:half], d_value[half:])

    h2_move.finish()
    dy_move.forward()
    dy_move.finish()
    reduce_far.wait()
    gwo_ref[...] = part[0] + far_buf[...]


def tail_kernel(dqkv_ref, gb_ref, h1_ref, wq_ref, x_ref, dx1t_ref, sums_ref, vec_ref, bu_ref, wu_ref, wd_ref, h2_own, h2_far, dy_own, dy_far,
                gx_ref, gwq_ref, gb_out, sums_out, gwu_ref, gbu_ref, gwd_ref,
                part, near_buf, far_buf, gb_buf, sums_mine, sums_buf, gx_seq, h2_all, dy_all, acc_up, acc_bias,
                load_sem, red_send, red_recv, small_send, small_recv, send_sem, recv_sem):
    me = lax.axis_index('tp')
    tp, chunk, width = gx_ref.shape
    group = dqkv_ref.shape[1]
    seq_len = tp * chunk
    greet(me)
    loads = []
    for m in range(tp):
        loads.append(pltpu.make_async_copy(h2_own if m == 0 else h2_far.at[m - 1], h2_all.at[m], load_sem.at[0, m]))
        loads.append(pltpu.make_async_copy(dy_own if m == 0 else dy_far.at[m - 1], dy_all.at[m], load_sem.at[1, m]))
    for load in loads:
        load.start()
    gb_moves = [remote(gb_ref.at[m], gb_buf.at[m - 1], small_send.at[0, m], small_recv.at[0, m], me ^ m) for m in (1, 2, 3)]
    for move in gb_moves:
        move.start()
    reduce_near = [remote(part.at[src], near_buf.at[i], red_send.at[i], red_recv.at[i], me ^ 1) for i, src in enumerate((1, 3))]
    reduce_far = remote(part.at[2], far_buf, red_send.at[2], red_recv.at[2], me ^ 2)
    part[...] = dot(dqkv_ref[...].reshape(tp * group, seq_len), h1_ref[...]).reshape(part.shape)
    cols = vec_ref[...].T
    gain, bias = cols[:, 0:1], cols[:, 1:2]
    for copy in reduce_near:
        copy.start()
    d_h1 = dot_tn(wq_ref[...].reshape(tp * group, width), dqkv_ref[...].reshape(tp * group, seq_len))
    _, x_hat, inv_std = layer_norm_rows(x_ref[...].T.astype(F32), gain, bias)
    grad_x = (dx1t_ref[...] + layer_norm_rows_grad(d_h1, x_hat, inv_std, gain)).astype(BF16)
    gx_seq[...] = grad_x.T
    for copy in reduce_near:
        copy.wait()
    part[0] += near_buf[0]
    part[2] += near_buf[1]
    sums = [jnp.sum(d_h1 * x_hat, axis=1, keepdims=True), jnp.sum(d_h1, axis=1, keepdims=True)]
    ln1 = jnp.concatenate(sums + [jnp.zeros((width, 126), F32)], axis=1).T
    sums_mine[...] = jnp.concatenate([sums_ref[:4], ln1[:4]], axis=0)
    gx_ref[me] = gx_seq[pl.ds(pl.multiple_of(me * chunk, chunk), chunk)]
    reduce_far.start()
    gx_move = FromSequence(gx_seq, gx_ref, send_sem, recv_sem, me, chunk)
    gx_move.start()
    sums_moves = [remote(sums_mine, sums_buf.at[m - 1], small_send.at[1, m], small_recv.at[1, m], me ^ m) for m in (1, 2, 3)]
    for move in sums_moves:
        move.start()
    for load in loads:
        load.wait()
    acc_up[...] = jnp.zeros_like(acc_up)
    acc_bias[...] = jnp.zeros_like(acc_bias)
    gwd_ref[...] = jnp.zeros_like(gwd_ref)
    wu_t = wu_ref[...].T
    bu_col = bu_ref[...].T[:, :1]

    @pl.loop(0, tp)
    def _(m):
        act, slope = gelu(dot_nt(wu_t, h2_all[m]) + bu_col)
        d_pre = dot_nt(wd_ref[...], dy_all[m]) * slope
        lanes = d_pre[:, :128]
        for i in range(1, seq_len // 128):
            lanes = lanes + d_pre[:, i * 128:(i + 1) * 128]
        acc_bias[...] += lanes
        gwd_ref[...] += dot(act, dy_all[m])
        acc_up[...] += dot(d_pre.astype(BF16), h2_all[m])

    gwu_ref[...] = acc_up[...].T
    gbu_ref[...] = jnp.broadcast_to(jnp.sum(acc_bias[...], axis=1, keepdims=True), acc_bias.shape).T[:8]
    for move in gb_moves + sums_moves:
        move.wait()
    gb_out[...] = gb_ref[0] + gb_buf[0] + (gb_buf[1] + gb_buf[2])
    sums_out[...] = sums_mine[...] + sums_buf[0] + (sums_buf[1] + sums_buf[2])
    reduce_far.wait()
    gwq_ref[...] = part[0] + far_buf[...]
    gx_move.wait()


VMEM_SPEC = pl.BlockSpec(memory_space=pltpu.VMEM)
ANY_SPEC = pl.BlockSpec(memory_space=pl.ANY)


def shape(dims, dtype=BF16):
    return jax.ShapeDtypeStruct(dims, dtype)


def single_call(kernel, name, collective_id, ins, in_any, outs, out_any, scratch):
    dma = pltpu.SemaphoreType.DMA
    return pl.pallas_call(
        kernel,
        out_shape=outs,
        in_specs=[ANY_SPEC if i in in_any else VMEM_SPEC for i in range(len(ins))],
        out_specs=[ANY_SPEC if i in out_any else VMEM_SPEC for i in range(len(outs))],
        scratch_shapes=[dma(s) if isinstance(s, tuple) else pltpu.VMEM(s.shape, s.dtype) for s in scratch],
        compiler_params=pltpu.CompilerParams(collective_id=collective_id, has_side_effects=True, vmem_limit_bytes=60 << 20),
        name=name,
    )(*ins)


def solution(mesh):
    tp = mesh.shape['tp']
    act_spec = P('dp', 'tp', None)
    rep_vec = P(None)
    part_vec = P('dp')
    in_specs = (act_spec, act_spec, P('dp', None), rep_vec, rep_vec, P(None, None, 'tp', None), P(None, 'tp', None),
                P('tp', None, None), rep_vec, rep_vec, rep_vec, P(None, 'tp'), P('tp'), P('tp', None), rep_vec)
    out_specs = (act_spec, act_spec, part_vec, part_vec, P('dp', None, 'tp', None), P('dp', 'tp', None),
                 P(('dp', 'tp'), None, None), part_vec, part_vec, part_vec, P('dp', 'tp'), P(('dp', 'tp')),
                 P(('dp', 'tp'), None), part_vec)

    def device_step(x_in, grad_y, pad_mask, ln1_gain, ln1_bias, w_qkv, b_qkv, w_out, b_out, ln2_gain, ln2_bias, w_up, b_up, w_down, b_down):
        me = lax.axis_index('tp')
        seq_len = pad_mask.shape[1]
        local_heads, head_dim = w_qkv.shape[2:]
        width = x_in.shape[2]
        heads = local_heads * tp
        q_scale = head_dim ** -0.5
        cos_tab, sin_tab = rope_tables(seq_len, head_dim)
        length = jnp.sum((lax.dynamic_index_in_dim(pad_mask, me, 0) > 0).astype(jnp.int32), axis=1)
        qkv_rows = 3 * local_heads * head_dim
        half_dim = head_dim // 2
        key_bias = jnp.where(jnp.arange(seq_len) < length[0], 0.0, NEG_LARGE).astype(BF16)
        key_bias = jnp.zeros((half_dim, seq_len), BF16).at[0].set(key_bias)
        wq_own = w_qkv.transpose(0, 2, 3, 1).reshape(qkv_rows, width)
        bq_own = jnp.broadcast_to(b_qkv.reshape(1, qkv_rows), (8, qkv_rows))
        wo_own = w_out.reshape(local_heads * head_dim, width)
        bu_own = jnp.broadcast_to(b_up[None], (8,) + b_up.shape)
        (x_full, wq_all, h1, q_ext, k_ext, v_heads, attn_o, attn_wide, lse, wo_all, wu_all, wd_all, bu_all, dy_full) = forward_call(
            x_in, wq_own, bq_own, key_bias, ln1_gain[None], ln1_bias[None], cos_tab[:half_dim], sin_tab[:half_dim], wo_own, w_up, w_down, bu_own, grad_y, local_heads, head_dim)
        chunk = seq_len // tp
        ff = w_up.shape[1]
        rows = heads * head_dim
        vec = jnp.stack([b_out, ln2_gain, ln2_bias, b_down, ln1_gain, ln1_bias, b_out, b_out])
        bu_full = jnp.concatenate([bu_own[None], bu_all])
        o_flat = attn_o.reshape(rows, seq_len)
        ins = (x_full, o_flat, wo_own, wo_all.reshape(-1, width), vec, bu_full, dy_full, w_up, wu_all, w_down, wd_all)
        outs = [shape((tp, chunk, width)), shape((seq_len, width)), shape((width, seq_len), F32), shape((seq_len, width)), shape((rows, seq_len)), shape((8, width), F32)]
        scratch = [shape((tp,) + w_up.shape), shape((tp,) + w_down.shape), shape((tp, ff, seq_len), F32), shape((tp, ff, seq_len)), shape((seq_len, width)), (2, 4), (4,), (4,)]
        y_out, h2, dx1_t, dx1_b, d_o, mid_sums = single_call(middle_kernel, 'middle', 1, ins, (7, 8, 9, 10), outs, (), scratch)
        ins = (q_ext, k_ext, v_heads, d_o.reshape(heads, head_dim, seq_len), attn_wide, lse, cos_tab[:half_dim], sin_tab[:half_dim], o_flat, dx1_b, h2, dy_full)
        group = local_heads * head_dim
        outs = [shape((tp, 3, group, seq_len)), shape((tp, 3, group, 128), F32), shape((group, width), F32), shape((tp - 1, seq_len, width)), shape((tp - 1, seq_len, width))]
        scratch = [shape((tp, group, width), F32), shape((2, group, width), F32), shape((group, width), F32), (3,), (3,), (2, 3), (2, 3)]
        dqkv, gb_wide, grad_w_out, h2_all, dy_all = single_call(functools.partial(backward_kernel, (local_heads, head_dim)), 'backward', 2, ins, (10, 11), outs, (3, 4), scratch)
        gb_part = jnp.broadcast_to(gb_wide[..., 0].reshape(tp, 1, qkv_rows), (tp, 8, qkv_rows))
        vec1 = jnp.stack([ln1_gain, ln1_bias] + [ln1_gain] * 6)
        ins = (dqkv.reshape(tp, qkv_rows, seq_len), gb_part, h1, wq_all, x_full, dx1_t, mid_sums, vec1, bu_own, w_up, w_down, h2, h2_all, dy_full, dy_all)
        outs = [shape((tp, chunk, width)), shape((qkv_rows, width), F32), shape((8, qkv_rows), F32), shape((8, width), F32), shape(w_up.shape, F32), shape((8, ff), F32), shape(w_down.shape, F32)]
        scratch = [shape((tp, qkv_rows, width), F32), shape((2, qkv_rows, width), F32), shape((qkv_rows, width), F32), shape((3, 8, qkv_rows), F32), shape((8, width), F32), shape((3, 8, width), F32),
                   shape((seq_len, width)), shape((tp, seq_len, width)), shape((tp, seq_len, width)), shape((ff, width), F32), shape((ff, 128), F32), (2, 4), (3,), (3,), (2, 4), (2, 4), (4,), (4,)]
        grad_x, grad_w_qkv, grad_b_qkv, sums, grad_w_up, grad_b_up, grad_w_down = single_call(tail_kernel, 'tail', 3, ins, (11, 12, 13, 14), outs, (), scratch)
        grad_w_qkv = grad_w_qkv.reshape(3, local_heads, head_dim, width).transpose(0, 3, 1, 2)
        grad_b_qkv = grad_b_qkv[0].reshape(3, local_heads, head_dim)
        grad_w_out = grad_w_out.reshape(local_heads, head_dim, width)
        return (y_out, grad_x, sums[4], sums[5], grad_w_qkv, grad_b_qkv, grad_w_out, sums[3],
                sums[1], sums[2], grad_w_up, grad_b_up[0], grad_w_down, sums[0])

    return jax.shard_map(device_step, mesh=mesh, in_specs=in_specs, out_specs=out_specs, check_vma=False)
```

profile of v0, /device:TPU:0, one launch (start us, length us, event | category | flops | bytes accessed | tf_op | source)
XLA Modules:
  0.0 299.9 jit_solution(15263694669822431542)
XLA Ops:
  0.6 1.4 fusion.3
  2.0 0.7 fusion.4
  2.7 0.6 scatter.4.mask_ref
  3.3 0.1 iota_multiply_fusion
  3.4 0.9 fusion.2
  4.3 1.3 broadcast_in_dim.41.gain_ref
  5.6 1.3 broadcast_in_dim.42.bias_ref
  6.8 1.3 broadcast_in_dim.43.bu_ref
  8.1 0.7 copy.30
  8.8 0.1 broadcast_in_dim.37
  8.9 0.6 broadcast_in_dim.38.bq_ref
  9.5 0.0 copy-start.8
  9.5 0.0 copy-start.9
  9.5 0.0 copy-start.10
  9.5 0.0 copy-start.11
  9.5 0.0 copy-start.12
  9.5 0.0 copy-start.6
  9.5 0.0 copy-start.7
  9.6 95.4 %forward.1 = (bf16[1024,640]{1,0:T(8,128)(2,1)}, bf16[4,480,640]{2,1,0:T(8,128)(2,1)}, bf16[1024,640]{1,0:T(8,128)(2,1)}, bf16[20,48,1024]{2,1,0:T(8,128)(2,1)},...) custom-call(bf16[4,256,640]{2,1,0:T(8,128)(2,1)} %x_ref.1, ...), custom_call_target="tpu_custom_call" | custom-call | tf_op jit(solution)/shard_map/forward/pallas_call | solution.py:193
  104.9 0.0 copy-done.8
  104.9 1.5 pad_maximum_fusion.bu_ref
  106.4 0.0 copy-done.9
  106.4 0.0 copy-done.10
  106.4 0.0 copy-done.11
  106.5 0.0 copy-done.12
  106.5 0.0 copy-done.6
  106.5 0.0 copy-done.7
  106.5 0.6 stack.16.vec_ref
  107.1 40.2 %middle.1 = (bf16[4,256,640]{2,1,0:T(8,128)(2,1)}, bf16[1024,640]{1,0:T(8,128)(2,1)}, f32[640,1024]{1,0:T(8,128)}, bf16[1024,640]{1,0:T(8,128)(2,1)}, bf16[640,1024]{1,0:T(8,128)(2,1)}, /*index=5*/f32[8,640]{1,0:T(8,128)}) custom-call(bf16[1024,640]{1,0:T(8,128)(2,1)} %get-tuple-element.58.x_ref, bf16[640,1024]{1,0:T(8,128)(2,1)} %bitcast.12, ...), custom_call_target="tpu_custom_call" | custom-call | tf_op jit(solution)/shard_map/middle/pallas_call | solution.py:466
  147.4 74.9 %backward.1 = (bf16[4,3,160,1024]{3,2,1,0:T(8,128)(2,1)}, f32[4,3,160,128]{3,2,1,0:T(8,128)}, f32[160,640]{1,0:T(8,128)}, bf16[3,1024,640]{2,1,0:T(8,128)(2,1)}, bf16[3,1024,640]{2,1,0:T(8,128)(2,1)}) custom-call(bf16[20,48,1024]{2,1,0:T(8,128)(2,1)} %get-tuple-element.66.q_all, bf16[20,48,1024]{2,1,0:T(8,128)(2,1)} %get-tuple-element.67.k_all, ...), custom_call_target="tpu_custom_call" | custom-call | tf_op jit(solution)/shard_map/backward/pallas_call | solution.py:466
  222.3 1.7 slice_reduce_fusion
  224.0 0.1 broadcast_in_dim.44
  224.0 0.6 broadcast_in_dim.45.gb_ref
  224.7 0.6 stack.17.vec_ref
  225.3 0.0 copy-start.2
  225.3 62.7 %tail.1 = (bf16[4,256,640]{2,1,0:T(8,128)(2,1)}, f32[480,640]{1,0:T(8,128)}, f32[8,480]{1,0:T(8,128)}, f32[8,640]{1,0:T(8,128)}, f32[640,640]{1,0:T(8,128)}, /*index=5*/f32[8,640]{1,0:T(8,128)}, f32[640,640]{1,0:T(8,128)}) custom-call(bf16[4,480,1024]{2,1,0:T(8,128)(2,1)} %bitcast.14, f32[4,8,480]{2,1,0:T(8,128)} %broadcast_in_dim.45.gb_ref, ...), custom_call_target="tpu_custom_call" | custom-call | tf_op jit(solution)/shard_map/tail/pallas_call | solution.py:466
  288.0 1.7 slice_reduce_fusion.1
  289.8 0.7 slice_reduce_fusion.8
  290.5 0.1 reshape_squeeze.4
  290.6 0.6 copy.31
  291.2 0.0 copy-done.2
  291.2 0.0 copy-start.3
  291.2 1.1 copy.38
  292.2 0.7 copy-done.3
  293.0 0.0 copy-start.4
  293.0 1.1 copy.39
  294.0 0.7 copy-done.4
  294.7 0.0 copy-start.5
  294.7 0.0 copy-start.1
  294.7 1.0 copy.40
  295.8 0.2 copy-done.5
  296.0 0.8 copy.41
  296.7 0.0 copy-done.1
  296.7 0.0 copy-start
  296.7 1.2 copy.42
  297.9 0.9 copy-done
  298.8 1.2 copy.43
  (6 shorter events, 0.0 us)
Async XLA Ops:
  9.5 95.4 %copy-start.8 = (f32[640]{0:T(1024)S(1)}, f32[640]{0:T(1024)}, u32[]{:S(2)}) copy-start(f32[640]{0:T(1024)} %param.29) | copy-start | bytes 7684
  9.5 96.9 %copy-start.9 = (f32[640]{0:T(1024)S(1)}, f32[640]{0:T(1024)}, u32[]{:S(2)}) copy-start(f32[640]{0:T(1024)} %param.25) | copy-start | bytes 7684
  9.5 96.9 %copy-start.10 = (f32[640]{0:T(1024)S(1)}, f32[640]{0:T(1024)}, u32[]{:S(2)}) copy-start(f32[640]{0:T(1024)} %param.26) | copy-start | bytes 7684
  9.5 96.9 %copy-start.11 = (f32[640]{0:T(1024)S(1)}, f32[640]{0:T(1024)}, u32[]{:S(2)}) copy-start(f32[640]{0:T(1024)} %param.27) | copy-start | bytes 7684
  9.5 96.9 %copy-start.12 = (f32[640]{0:T(1024)S(1)}, f32[640]{0:T(1024)}, u32[]{:S(2)}) copy-start(f32[640]{0:T(1024)} %param.31) | copy-start | bytes 7684
  9.5 97.0 %copy-start.6 = (f32[1,640]{1,0:T(1,128)S(1)}, f32[1,640]{1,0:T(1,128)}, u32[]{:S(2)}) copy-start(f32[1,640]{1,0:T(1,128)} %broadcast_in_dim.41.gain_ref) | copy-start | bytes 7684
  9.5 97.0 %copy-start.7 = (f32[1,640]{1,0:T(1,128)S(1)}, f32[1,640]{1,0:T(1,128)}, u32[]{:S(2)}) copy-start(f32[1,640]{1,0:T(1,128)} %broadcast_in_dim.42.bias_ref) | copy-start | bytes 7684
  225.3 65.8 %copy-start.2 = (bf16[4,256,640]{2,1,0:T(8,128)(2,1)S(1)}, bf16[4,256,640]{2,1,0:T(8,128)(2,1)}, u32[]{:S(2)}) copy-start(bf16[4,256,640]{2,1,0:T(8,128)(2,1)} %get-tuple-element.141) | copy-start | bytes 3932164
  291.2 1.8 copy-start.3
  293.0 1.8 copy-start.4
  294.7 1.3 copy-start.5
  294.7 2.0 copy-start.1
  296.7 2.0 copy-start
where the time goes:
time: 301 us; the launch traced here: 300 us
  Pallas kernels  273 us (91%)
  local copies, waits for them, and re-layouts  21.5 us (7%)
  other arithmetic  4.48 us (1%)
    pallas_call x3, Pallas kernels, single_call(): pl.pallas_call(kernel, out_shape=outs, in_specs=[ANY_SPEC if i in in_any...  178 us
    pallas_call x1, Pallas kernels, forward_call(): pl.pallas_call(functools.partial(forward_kernel, (chunk, local_heads, hea...  95.4 us
    unnamed x34, local copies, waits for them, and re-layouts  10.1 us

commit v1 on v0

v1 whole, which is shorter than its diff:
```python
import functools

import jax
import jax.numpy as jnp
import numpy as np
from jax import lax
from jax.experimental import pallas as pl
from jax.experimental.pallas import tpu as pltpu
from jax.sharding import PartitionSpec as P

LN_EPS = 1e-5
ROPE_BASE = 10000.0
INV_SQRT2 = 0.7071067811865476
INV_SQRT_2PI = 0.3989422804014327
NEG_LARGE = -1e30
F32 = jnp.float32
BF16 = jnp.bfloat16
MESH = pl.DeviceIdType.MESH


def dot(lhs, rhs):
    return jnp.dot(lhs, rhs, preferred_element_type=F32)


def layer_norm(values, ln_gain, ln_bias):
    centered = values - jnp.mean(values, axis=-1, keepdims=True)
    inv_std = lax.rsqrt(jnp.mean(centered * centered, axis=-1, keepdims=True) + LN_EPS)
    x_hat = centered * inv_std
    return x_hat * ln_gain + ln_bias, x_hat, inv_std


def rope_tables(seq_len, head_dim):
    half_dim = head_dim // 2
    inv_freq = np.float32(ROPE_BASE) ** (np.float32(-2.0) * np.arange(half_dim, dtype=np.float32) / np.float32(head_dim))
    angles = inv_freq[:, None] * np.arange(seq_len, dtype=np.float32)[None, :]
    return np.cos(angles), np.sin(angles)


def remote(src, dst, send_sem, recv_sem, device):
    return pltpu.make_async_remote_copy(src_ref=src, dst_ref=dst, send_sem=send_sem, recv_sem=recv_sem, device_id={'tp': device}, device_id_type=MESH)


def greet(me):
    barrier = pltpu.get_barrier_semaphore()
    for mask in (1, 2, 3):
        pl.semaphore_signal(barrier, inc=1, device_id={'tp': me ^ mask}, device_id_type=MESH)
    pl.semaphore_wait(barrier, 3)


class Gather:
    def __init__(self, src, dst, base, send_sem, recv_sem, me):
        self.near = remote(src, dst.at[1 - base], send_sem.at[0], recv_sem.at[0], me ^ 1)
        self.far = remote(src, dst.at[2 - base], send_sem.at[1], recv_sem.at[1], me ^ 2)
        self.relay = remote(dst.at[2 - base], dst.at[3 - base], send_sem.at[2], recv_sem.at[2], me ^ 1)

    def start(self):
        self.far.start()
        self.near.start()

    def forward(self):
        self.far.wait_recv()
        self.relay.start()

    def finish(self):
        self.near.wait()
        self.far.wait_send()
        self.relay.wait()


def layer_norm_rows(values, ln_gain, ln_bias):
    centered = values - jnp.mean(values, axis=0, keepdims=True)
    inv_std = lax.rsqrt(jnp.mean(centered * centered, axis=0, keepdims=True) + LN_EPS)
    x_hat = centered * inv_std
    return x_hat * ln_gain + ln_bias, x_hat, inv_std


def layer_norm_rows_grad(d_out, x_hat, inv_std, ln_gain):
    d_hat = d_out * ln_gain
    return inv_std * (d_hat - jnp.mean(d_hat, axis=0, keepdims=True) - x_hat * jnp.mean(d_hat * x_hat, axis=0, keepdims=True))


def dot_tn(lhs, rhs):
    return lax.dot_general(lhs, rhs, (((0,), (0,)), ((), ())), preferred_element_type=F32)


def dot_nt(lhs, rhs):
    return lax.dot_general(lhs, rhs, (((1,), (1,)), ((), ())), preferred_element_type=F32)


def gelu(pre_act):
    half_erf = 0.5 * (1.0 + lax.erf(pre_act * INV_SQRT2))
    act = (pre_act * half_erf).astype(BF16)
    return act, half_erf + pre_act * jnp.exp(-0.5 * pre_act * pre_act) * INV_SQRT_2PI


class Copies:
    def __init__(self, copies):
        self.copies = copies

    def start(self):
        for copy in self.copies:
            copy.start()

    def wait(self):
        for copy in self.copies:
            copy.wait()

    def wait_recv(self):
        for copy in self.copies:
            copy.wait_recv()

    def wait_send(self):
        for copy in self.copies:
            copy.wait_send()


def rows_of(owner, chunk):
    return pl.ds(pl.multiple_of(owner * chunk, chunk), chunk)


def to_sequence(src, dst, send_sem, recv_sem, me, chunk):
    return Copies([remote(src.at[me ^ mask], dst.at[rows_of(me, chunk)], send_sem.at[mask], recv_sem.at[mask], me ^ mask) for mask in (2, 3, 1)])


def from_sequence(src, dst, send_sem, recv_sem, me, chunk):
    return Copies([remote(src.at[rows_of(me ^ mask, chunk)], dst.at[me], send_sem.at[mask], recv_sem.at[mask], me ^ mask) for mask in (2, 3, 1)])


def lane_sum(value):
    return jnp.sum(value, axis=1, keepdims=True)


def forward_kernel(dims, x_ref, wq_ref, bq_ref, mask_ref, vec_ref, cos_ref, sin_ref, wo_ref, wu_ref, wd_ref,
                   x_out, wq_out, h1_out, q_out, k_out, v_out, o_out, wide_out, lse_out, wo_all, wu_all, wd_all, vec_all,
                   x_full, wq_all, h1_ref, q_all, k_all, v_all, o_ref, wide_ref, lse_ref, h1t_ref, bq_all,
                   own_sem, once_sem, store_sem, send_sem, recv_sem):
    chunk, local_heads, head_dim = dims
    me = lax.axis_index('tp')
    half = head_dim // 2
    seq_len = mask_ref.shape[1]
    greet(me)
    x_move = to_sequence(x_ref, x_full, send_sem.at[0], recv_sem.at[0], me, chunk)
    wq = Gather(wq_ref, wq_all, 0, send_sem.at[1], recv_sem.at[1], me)
    bq = Gather(bq_ref, bq_all, 0, send_sem.at[2], recv_sem.at[2], me)
    others = [Gather(src, dst, 1, send_sem.at[3 + i], recv_sem.at[3 + i], me) for i, (src, dst) in enumerate(((vec_ref, vec_all), (wo_ref, wo_all), (wu_ref, wu_all), (wd_ref, wd_all)))]
    x_move.start()
    bq.start()
    wq.start()
    own_wq = pltpu.make_async_copy(wq_ref, wq_all.at[0], own_sem)
    own_wq.start()
    for move in others:
        move.start()
    own_rows = rows_of(me, chunk)
    x_full[own_rows] = x_ref[me]
    bq_all[0] = bq_ref[...]
    valid = mask_ref[pl.ds(me, 1)] > 0
    first = lax.broadcasted_iota(jnp.int32, (half, seq_len), 0) == 0
    ones = first.astype(F32).astype(BF16)
    key_bias = jnp.where(first, jnp.where(valid, 0.0, NEG_LARGE), 0.0).astype(BF16)
    x_move.wait_recv()
    x_f = x_full[...].astype(F32)
    h1, _, _ = layer_norm(x_f, vec_ref[4:5], vec_ref[5:6])
    h1 = h1.astype(BF16)
    h1_ref[...] = h1
    h1t_ref[...] = h1.T
    once = Copies([pltpu.make_async_copy(src, dst, once_sem.at[i]) for i, (src, dst) in enumerate(((x_full, x_out), (h1_ref, h1_out), (wq_all, wq_out)))])
    for copy in once.copies[:2]:
        copy.start()
    own_wq.wait()

    def stores(m):
        heads = pl.ds(m * local_heads, local_heads)
        pairs = ((q_all, q_out), (k_all, k_out), (v_all, v_out), (o_ref, o_out), (wide_ref, wide_out), (lse_ref, lse_out))
        return Copies([pltpu.make_async_copy(src.at[heads], dst.at[heads], store_sem.at[i, m]) for i, (src, dst) in enumerate(pairs)])

    @pl.loop(0, 4)
    def _(m):
        @pl.when(m == 1)
        def _():
            bq.near.wait_recv()
            wq.near.wait_recv()

        @pl.when(m == 2)
        def _():
            bq.forward()
            wq.forward()

        @pl.when(m == 3)
        def _():
            bq.relay.wait_recv()
            wq.relay.wait_recv()
            once.copies[2].start()

        bias = bq_all[m].T[:, :1]
        qkv = dot(wq_all[m], h1t_ref[...]) + bias
        cos, sin = cos_ref[...], sin_ref[...]
        group = local_heads * head_dim
        for j in range(local_heads):
            head = m * local_heads + j
            for which, (dst, scale, extra) in enumerate(((q_all, head_dim ** -0.5, ones), (k_all, None, key_bias))):
                rows = qkv[which * group + j * head_dim:which * group + (j + 1) * head_dim]
                rows = rows * scale if scale is not None else rows
                low, high = rows[:half], rows[half:]
                dst[head, :half] = (low * cos - high * sin).astype(BF16)
                dst[head, half:head_dim] = (high * cos + low * sin).astype(BF16)
                dst[head, head_dim:] = extra
            v_all[head] = qkv[2 * group + j * head_dim:2 * group + (j + 1) * head_dim].astype(BF16)

        @pl.loop(0, local_heads)
        def _(j):
            head = m * local_heads + j
            scores = dot(k_all[head].T, q_all[head])
            top = jnp.max(scores, axis=0, keepdims=True)
            weights = jnp.exp(scores - top)
            total = jnp.sum(weights, axis=0, keepdims=True)
            out = dot(v_all[head], weights.astype(BF16)) / total
            o_ref[head] = out.astype(BF16)
            wide_ref[head] = out
            lse_ref[head] = top + jnp.log(total)

        stores(m).start()

    x_move.wait_send()
    for move in (bq, wq):
        move.near.wait_send()
        move.far.wait_send()
        move.relay.wait_send()
    for move in others:
        move.forward()
    for m in range(4):
        stores(m).wait()
    once.wait()
    for move in others:
        move.finish()


def middle_kernel(x_ref, o_ref, wo_ref, wo_far_ref, vec_ref, vec_far_ref, dy_ref, wu_own, wu_far, wd_own, wd_far,
                  y_ref, h2_ref, dx1t_ref, dx1b_ref, do_ref, sums_ref, dy_full, h2_all,
                  wu_all, wd_all, vec_all, slope_ref, act_ref, load_sem, send_sem, recv_sem):
    me = lax.axis_index('tp')
    tp, chunk, width = dy_ref.shape
    ff = wu_own.shape[1]
    greet(me)
    dy_move = to_sequence(dy_ref, dy_full, send_sem.at[0], recv_sem.at[0], me, chunk)
    dy_move.start()
    loads = []
    for m in range(tp):
        wu_src = wu_own if m == 0 else wu_far.at[m - 1]
        wd_src = wd_own if m == 0 else wd_far.at[m - 1]
        loads.append((pltpu.make_async_copy(wu_src, wu_all.at[m], load_sem.at[0, m]), pltpu.make_async_copy(wd_src, wd_all.at[m], load_sem.at[1, m])))
    for load, _ in loads:
        load.start()
    for _, load in loads:
        load.start()
    own_rows = rows_of(me, chunk)
    dy_full[own_rows] = dy_ref[me]
    vec_all[0] = vec_ref[...]
    vec_all[1:] = vec_far_ref[...]
    cols = vec_ref[...].T
    b_out, gain, bias, b_down = (cols[:, i:i + 1] for i in range(4))
    rows = wo_ref.shape[0]
    attn = dot_tn(wo_ref[...], o_ref[:rows]) + dot_tn(wo_far_ref[...], o_ref[rows:])
    x1 = (x_ref[...].T.astype(F32) + (attn + b_out)).astype(BF16).astype(F32)
    h2_f, x_hat, inv_std = layer_norm_rows(x1, gain, bias)
    h2 = h2_f.astype(BF16)
    h2_ref[...] = h2.T
    for load, _ in loads:
        load.wait()
    h2_move = Gather(h2_ref.at[:tp * chunk // 2], h2_all, 1, send_sem.at[1], recv_sem.at[1], me)

    @pl.loop(0, tp)
    def _(m):
        @pl.when(m == 1)
        def _():
            h2_move.start()

        pre_act = dot_tn(wu_all[m], h2) + vec_all[m].T[:, 6:7]
        act, slope = gelu(pre_act)
        act_ref[m] = act
        slope_ref[m] = slope

    for _, load in loads:
        load.wait()
    mlp = dot_tn(wd_all[...].reshape(tp * ff, width), act_ref[...].reshape(tp * ff, tp * chunk))
    y_ref[...] = (x1 + (mlp + b_down)).astype(BF16).T
    dy_move.wait_recv()
    dy_t = dy_full[...].T
    dy_f = dy_t.astype(F32)

    @pl.loop(0, tp)
    def _(m):
        act_ref[m] = (dot(wd_all[m], dy_t) * slope_ref[m]).astype(BF16)

    d_h2 = dot(wu_all[0], act_ref[0])
    for m in range(1, tp):
        d_h2 = d_h2 + dot(wu_all[m], act_ref[m])
    d_x1 = dy_f + layer_norm_rows_grad(d_h2, x_hat, inv_std, gain)
    dx1t_ref[...] = d_x1
    d_x1_b = d_x1.astype(BF16)
    dx1b_ref[...] = d_x1_b.T
    do_ref[:rows] = dot(wo_ref[...], d_x1_b).astype(BF16)
    do_ref[rows:] = dot(wo_far_ref[...], d_x1_b).astype(BF16)
    h2_move.forward()
    sums = [lane_sum(dy_f), lane_sum(d_h2 * x_hat), lane_sum(d_h2), lane_sum(d_x1)]
    sums_ref[...] = jnp.concatenate(sums + [jnp.zeros((width, 124), F32)], axis=1).T[:8]
    dy_move.wait_send()
    h2_move.finish()


def backward_kernel(dims, q_in, k_in, v_in, do_in, wide_in, lse_in, cos_ref, sin_ref, o_ref, dx1b_ref, h1_ref, h2_ref, dy_ref, dy_full, y_ref,
                    dqkv_ref, gb_ref, gwo_ref, far_qk, h2_all, dy_all, y_out,
                    q_all, k_all, v_all, do_ref, wide_ref, lse_ref, part, near_buf, far_buf, part_qk, near_qk,
                    load_sem, own_sem, red_send, red_recv, h2_send, h2_recv, dy_send, dy_recv, y_send, y_recv):
    local_heads, head_dim = dims
    me = lax.axis_index('tp')
    tp, chunk, width = dy_ref.shape
    half = head_dim // 2
    group = local_heads * head_dim

    def loads(m):
        heads = pl.ds(m * local_heads, local_heads)
        pairs = ((q_in, q_all), (k_in, k_all), (v_in, v_all), (do_in, do_ref), (wide_in, wide_ref), (lse_in, lse_ref))
        return Copies([pltpu.make_async_copy(src.at[heads], dst.at[heads], load_sem.at[i, m]) for i, (src, dst) in enumerate(pairs)])

    greet(me)
    for m in range(tp - 1, -1, -1):
        loads(m).start()
    mine, across, partner = rows_of(me, chunk), rows_of(me ^ 2, chunk), me ^ 1
    h2_move = Gather(h2_ref.at[tp * chunk // 2:], h2_all, 1, h2_send, h2_recv, me)
    y_move = from_sequence(y_ref, y_out, y_send, y_recv, me, chunk)
    dy_near = Copies([remote(src, dst, dy_send.at[i], dy_recv.at[i], partner) for i, (src, dst) in enumerate((
        (dy_full, dy_all.at[0]), (dy_ref.at[me ^ 2], dy_all.at[2, mine]), (dy_ref.at[me ^ 3], dy_all.at[1, mine])))])
    dy_far = Copies([remote(dy_ref.at[me ^ i], dy_all.at[1 + i, mine], dy_send.at[3 + i], dy_recv.at[3 + i], me ^ 2) for i in (0, 1)])
    dy_relay = Copies([remote(dy_all.at[1 + i, across], dy_all.at[2 - i, across], dy_send.at[5 + i], dy_recv.at[5 + i], partner) for i in (0, 1)])
    own = Copies([pltpu.make_async_copy(dy_ref.at[me ^ 2], dy_all.at[1, mine], own_sem.at[0]), pltpu.make_async_copy(dy_ref.at[me ^ 3], dy_all.at[2, mine], own_sem.at[1]),
                  pltpu.make_async_copy(y_ref.at[mine], y_out.at[me], own_sem.at[2])])
    h2_move.start()
    dy_far.start()
    dy_near.start()
    own.start()
    reduce_near = Copies([remote(part.at[src], near_buf.at[i], red_send.at[i], red_recv.at[i], partner) for i, src in enumerate((1, 3))])
    reduce_far = remote(part.at[2], far_buf, red_send.at[2], red_recv.at[2], me ^ 2)
    qk_near = remote(part_qk.at[1], near_qk, red_send.at[3], red_recv.at[3], partner)
    qk_far = remote(part_qk.at[0], far_qk, red_send.at[4], red_recv.at[4], me ^ 2)
    part[...] = dot(o_ref[...], dx1b_ref[...]).reshape(part.shape)
    cos, sin = cos_ref[...], sin_ref[...]

    def store(m, j, which, low, high):
        grad = jnp.concatenate([low, high], axis=0)
        at = pl.ds(pl.multiple_of(j * head_dim, head_dim), head_dim)
        dqkv_ref[m, which, at] = grad.astype(BF16)
        gb_ref[m, which, at] = jnp.broadcast_to(lane_sum(grad), (head_dim, 128))

    def back(grad):
        low, high = grad[:half], grad[half:]
        return low * cos + high * sin, high * cos - low * sin

    @pl.loop(0, tp * local_heads)
    def _(step):
        m = tp - 1 - lax.div(step, local_heads)
        j = lax.rem(step, local_heads)
        head = m * local_heads + j

        @pl.when(j == 0)
        def _():
            loads(m).wait()

        @pl.when(step == 1)
        def _():
            reduce_near.start()

        @pl.when(step == 3)
        def _():
            reduce_near.wait()
            part[0] += near_buf[0]
            part[2] += near_buf[1]

        @pl.when(step == 4)
        def _():
            reduce_far.start()

        @pl.when(step == 7)
        def _():
            h2_move.forward()

        @pl.when(step == 10)
        def _():
            for i in (0, 1):
                part_qk[i] = dot(dqkv_ref[2 + i, :2].reshape(2 * group, tp * chunk), h1_ref[...])

        @pl.when(step == 11)
        def _():
            qk_near.start()

        @pl.when(step == 12)
        def _():
            qk_near.wait()
            part_qk[0] += near_qk[...]
            dy_far.wait_recv()
            dy_relay.start()

        @pl.when(step == 13)
        def _():
            qk_far.start()
            y_move.start()

        q, k, v, d_out = q_all[head], k_all[head], v_all[head], do_ref[head]
        delta = jnp.sum(d_out.astype(F32) * wide_ref[head], axis=0, keepdims=True)
        probs = jnp.exp(dot(k.T, q) - lse_ref[head])
        d_probs = dot(v.T, d_out)
        d_scores = (probs * (d_probs - delta)).astype(BF16)
        d_value = dot(probs.astype(BF16), d_out.T).T
        d_key = dot(d_scores, q[:head_dim].T).T
        d_query = dot(k[:head_dim], d_scores)
        low, high = back(d_query)
        scale = head_dim ** -0.5
        store(m, j, 0, low * scale, high * scale)
        low, high = back(d_key)
        store(m, j, 1, low, high)
        store(m, j, 2, d_value[:half], d_value[half:])

    own.wait()
    h2_move.finish()
    dy_near.wait()
    dy_far.wait_send()
    dy_relay.wait()
    reduce_far.wait()
    gwo_ref[...] = part[0] + far_buf[...]
    qk_far.wait()
    y_move.wait()


def tail_kernel(dqkv_ref, gb_ref, h1_ref, wq_in, x_in, dx1t_in, sums_ref, vec_ref, far_qk, wu_in, wd_in, h2_own, h2_low, h2_high, dy_own, dy_far,
                gx_ref, gwq_ref, gb_out, sums_out, gwu_ref, gbu_ref, gwd_ref,
                wq_ref, x_ref, dx1t_ref, wu_ref, wd_ref, part, part_v, near_buf, near_v, far_v, gb_buf, sums_mine, sums_buf, gx_seq, h2_all, dy_all, acc_up, acc_bias,
                first_sem, load_sem, red_send, red_recv, small_send, small_recv, send_sem, recv_sem):
    me = lax.axis_index('tp')
    tp, chunk, width = gx_ref.shape
    group = dqkv_ref.shape[1]
    split = group - part_v.shape[1]
    seq_len = tp * chunk
    first = [pltpu.make_async_copy(src, dst, first_sem.at[i]) for i, (src, dst) in enumerate(((wq_in, wq_ref), (x_in, x_ref), (dx1t_in, dx1t_ref), (wu_in, wu_ref), (wd_in, wd_ref)))]
    for load in first:
        load.start()
    greet(me)
    loads = []
    for m in range(tp):
        if m == 0:
            loads.append([pltpu.make_async_copy(h2_own, h2_all.at[0], load_sem.at[0, m])])
        else:
            loads.append([pltpu.make_async_copy(h2_low.at[m - 1], h2_all.at[m, :seq_len // 2], load_sem.at[0, m]), pltpu.make_async_copy(h2_high.at[m - 1], h2_all.at[m, seq_len // 2:], load_sem.at[2, m])])
        loads[m].append(pltpu.make_async_copy(dy_own if m == 0 else dy_far.at[m - 1], dy_all.at[m], load_sem.at[1, m]))
    for pair in loads:
        for load in pair:
            load.start()
    small = [remote(gb_ref.at[m], gb_buf.at[m - 1], small_send.at[0, m], small_recv.at[0, m], me ^ m) for m in (1, 2, 3)]
    for move in small:
        move.start()
    near = Copies([remote(part.at[1], near_buf, red_send.at[0], red_recv.at[0], me ^ 1), remote(part_v.at[1], near_v, red_send.at[1], red_recv.at[1], me ^ 1)])
    reduce_far = remote(part_v.at[0], far_v, red_send.at[2], red_recv.at[2], me ^ 2)
    h1 = h1_ref[...]
    part[...] = dot(dqkv_ref[:2].reshape(2 * group, seq_len), h1).reshape(part.shape)
    for i in (0, 1):
        part_v[i] = dot(dqkv_ref[2 + i, split:], h1)
    cols = vec_ref[...].T
    gain, bias = cols[:, 4:5], cols[:, 5:6]
    first[0].wait()
    near.start()
    d_h1 = dot_tn(wq_ref[...].reshape(tp * group, width), dqkv_ref[...].reshape(tp * group, seq_len))
    near.wait()
    part_v[0] += near_v[...]
    part[0] += near_buf[...]
    for load in first[1:]:
        load.wait()
    _, x_hat, inv_std = layer_norm_rows(x_ref[...].T.astype(F32), gain, bias)
    reduce_far.start()
    grad_x = (dx1t_ref[...] + layer_norm_rows_grad(d_h1, x_hat, inv_std, gain)).astype(BF16)
    gx_seq[...] = grad_x.T
    sums = [lane_sum(d_h1 * x_hat), lane_sum(d_h1)]
    ln1 = jnp.concatenate(sums + [jnp.zeros((width, 126), F32)], axis=1).T
    sums_mine[...] = jnp.concatenate([sums_ref[:4], ln1[:4]], axis=0)
    gx_ref[me] = gx_seq[rows_of(me, chunk)]
    gx_move = from_sequence(gx_seq, gx_ref, send_sem, recv_sem, me, chunk)
    gx_move.start()
    sums_moves = [remote(sums_mine, sums_buf.at[m - 1], small_send.at[1, m], small_recv.at[1, m], me ^ m) for m in (1, 2, 3)]
    for move in sums_moves:
        move.start()
    for pair in loads:
        for load in pair:
            load.wait()
    acc_up[...] = jnp.zeros_like(acc_up)
    acc_bias[...] = jnp.zeros_like(acc_bias)
    gwd_ref[...] = jnp.zeros_like(gwd_ref)
    wu_t = wu_ref[...].T
    bu_col = cols[:, 6:7]

    @pl.loop(0, tp)
    def _(m):
        act, slope = gelu(dot_nt(wu_t, h2_all[m]) + bu_col)
        d_pre = dot_nt(wd_ref[...], dy_all[m]) * slope
        lanes = d_pre[:, :128]
        for i in range(1, seq_len // 128):
            lanes = lanes + d_pre[:, i * 128:(i + 1) * 128]
        acc_bias[...] += lanes
        gwd_ref[...] += dot(act, dy_all[m])
        acc_up[...] += dot(d_pre.astype(BF16), h2_all[m])

    gwu_ref[...] = acc_up[...].T
    gbu_ref[...] = jnp.broadcast_to(lane_sum(acc_bias[...]), acc_bias.shape).T[:8]
    for move in small + sums_moves:
        move.wait()
    gb_out[...] = gb_ref[0] + gb_buf[0] + (gb_buf[1] + gb_buf[2])
    sums_out[...] = sums_mine[...] + sums_buf[0] + (sums_buf[1] + sums_buf[2])
    gwq_ref[:split] = part[0, :split] + far_qk[...]
    reduce_far.wait()
    gwq_ref[split:] = part[0, split:] + far_v[...]
    gx_move.wait()


VMEM_SPEC = pl.BlockSpec(memory_space=pltpu.VMEM)
ANY_SPEC = pl.BlockSpec(memory_space=pl.ANY)


def shape(dims, dtype=BF16):
    return jax.ShapeDtypeStruct(dims, dtype)


def single_call(kernel, name, collective_id, ins, in_any, outs, out_any, scratch):
    dma = pltpu.SemaphoreType.DMA
    return pl.pallas_call(
        kernel,
        out_shape=outs,
        in_specs=[ANY_SPEC if i in in_any else VMEM_SPEC for i in range(len(ins))],
        out_specs=[ANY_SPEC if i in out_any else VMEM_SPEC for i in range(len(outs))],
        scratch_shapes=[dma(s) if isinstance(s, tuple) else pltpu.VMEM(s.shape, s.dtype) for s in scratch],
        compiler_params=pltpu.CompilerParams(collective_id=collective_id, has_side_effects=True, vmem_limit_bytes=60 << 20),
        name=name,
    )(*ins)


def solution(mesh):
    tp = mesh.shape['tp']
    act_spec = P('dp', 'tp', None)
    rep_vec = P(None)
    part_vec = P('dp')
    in_specs = (act_spec, act_spec, P('dp', None), rep_vec, rep_vec, P(None, None, 'tp', None), P(None, 'tp', None),
                P('tp', None, None), rep_vec, rep_vec, rep_vec, P(None, 'tp'), P('tp'), P('tp', None), rep_vec)
    out_specs = (act_spec, act_spec, part_vec, part_vec, P('dp', None, 'tp', None), P('dp', 'tp', None),
                 P(('dp', 'tp'), None, None), part_vec, part_vec, part_vec, P('dp', 'tp'), P(('dp', 'tp')),
                 P(('dp', 'tp'), None), part_vec)

    def device_step(x_in, grad_y, pad_mask, ln1_gain, ln1_bias, w_qkv, b_qkv, w_out, b_out, ln2_gain, ln2_bias, w_up, b_up, w_down, b_down):
        seq_len = pad_mask.shape[1]
        local_heads, head_dim = w_qkv.shape[2:]
        chunk, width = x_in.shape[1:]
        ff = w_up.shape[1]
        heads = local_heads * tp
        group = local_heads * head_dim
        qkv_rows = 3 * group
        rows = heads * head_dim
        ext = head_dim + head_dim // 2
        dims = (local_heads, head_dim)
        cos_tab, sin_tab = (jnp.asarray(table) for table in rope_tables(seq_len, head_dim))
        wq_own = w_qkv.transpose(0, 2, 3, 1).reshape(qkv_rows, width)
        bq_own = jnp.broadcast_to(b_qkv.reshape(1, qkv_rows), (8, qkv_rows))
        wo_own = w_out.reshape(group, width)
        vec = jnp.stack([b_out, ln2_gain, ln2_bias, b_down, ln1_gain, ln1_bias, b_up, b_up])
        ins = (x_in, wq_own, bq_own, pad_mask, vec, cos_tab, sin_tab, wo_own, w_up, w_down)
        held = [shape((seq_len, width)), shape((tp, qkv_rows, width)), shape((seq_len, width)), shape((heads, ext, seq_len)), shape((heads, ext, seq_len)),
                shape((heads, head_dim, seq_len)), shape((heads, head_dim, seq_len)), shape((heads, head_dim, seq_len), F32), shape((heads, 1, seq_len), F32)]
        outs = held + [shape((tp - 1,) + wo_own.shape), shape((tp - 1,) + w_up.shape), shape((tp - 1,) + w_down.shape), shape((tp - 1,) + vec.shape, F32)]
        scratch = held + [shape((width, seq_len)), shape((tp,) + bq_own.shape, F32), (), (3,), (6, 4), (7, 4), (7, 4)]
        (x_full, wq_all, h1, q_ext, k_ext, v_heads, attn_o, attn_wide, lse, wo_all, wu_all, wd_all, vec_all) = single_call(
            functools.partial(forward_kernel, (chunk,) + dims), 'forward', 0, ins, (1, 7, 8, 9), outs, range(13), scratch)
        o_flat = attn_o.reshape(rows, seq_len)
        ins = (x_full, o_flat, wo_own, wo_all.reshape(-1, width), vec, vec_all, grad_y, w_up, wu_all, w_down, wd_all)
        half_rows = shape((tp - 1, seq_len // 2, width))
        outs = [shape((seq_len, width)), shape((seq_len, width)), shape((width, seq_len), F32), shape((seq_len, width)), shape((rows, seq_len)), shape((8, width), F32), shape((seq_len, width)), half_rows]
        scratch = [shape((tp,) + w_up.shape), shape((tp,) + w_down.shape), shape((tp, 8, width), F32), shape((tp, ff, seq_len), F32), shape((tp, ff, seq_len)), (2, 4), (2, 4), (2, 4)]
        y_seq, h2, dx1_t, dx1_b, d_o, mid_sums, dy_full, h2_low = single_call(middle_kernel, 'middle', 1, ins, (7, 8, 9, 10), outs, (7,), scratch)
        ins = (q_ext, k_ext, v_heads, d_o.reshape(heads, head_dim, seq_len), attn_wide, lse, cos_tab, sin_tab, o_flat, dx1_b, h1, h2, grad_y, dy_full, y_seq)
        outs = [shape((tp, 3, group, seq_len)), shape((tp, 3, group, 128), F32), shape((group, width), F32), shape((2 * group, width), F32), half_rows, shape((tp - 1, seq_len, width)), shape((tp, chunk, width))]
        scratch = [shape(a.shape, a.dtype) for a in ins[:6]] + [shape((tp, group, width), F32), shape((2, group, width), F32), shape((group, width), F32), shape((2, 2 * group, width), F32), shape((2 * group, width), F32),
                   (6, 4), (3,), (5,), (5,), (3,), (3,), (7,), (7,), (4,), (4,)]
        dqkv, gb_wide, grad_w_out, far_qk, h2_high, dy_all, y_out = single_call(functools.partial(backward_kernel, dims), 'backward', 2, ins, (0, 1, 2, 3, 4, 5, 11, 12, 13, 14), outs, (4, 5, 6), scratch)
        gb_part = jnp.broadcast_to(gb_wide[..., 0].reshape(tp, 1, qkv_rows), (tp, 8, qkv_rows))
        ins = (dqkv.reshape(tp, qkv_rows, seq_len), gb_part, h1, wq_all, x_full, dx1_t, mid_sums, vec, far_qk, w_up, w_down, h2, h2_low, h2_high, dy_full, dy_all)
        outs = [shape((tp, chunk, width)), shape((qkv_rows, width), F32), shape((8, qkv_rows), F32), shape((8, width), F32), shape(w_up.shape, F32), shape((8, ff), F32), shape(w_down.shape, F32)]
        scratch = [shape(ins[i].shape, ins[i].dtype) for i in (3, 4, 5, 9, 10)] + [
            shape((2, qkv_rows, width), F32), shape((2, group, width), F32), shape((qkv_rows, width), F32), shape((group, width), F32), shape((group, width), F32), shape((3, 8, qkv_rows), F32), shape((8, width), F32),
            shape((3, 8, width), F32), shape((seq_len, width)), shape((tp, seq_len, width)), shape((tp, seq_len, width)), shape((ff, width), F32), shape((ff, 128), F32),
            (5,), (3, 4), (3,), (3,), (2, 4), (2, 4), (4,), (4,)]
        grad_x, grad_w_qkv, grad_b_qkv, sums, grad_w_up, grad_b_up, grad_w_down = single_call(tail_kernel, 'tail', 3, ins, (3, 4, 5, 9, 10, 11, 12, 13, 14, 15), outs, (), scratch)
        grad_w_qkv = grad_w_qkv.reshape(3, local_heads, head_dim, width).transpose(0, 3, 1, 2)
        grad_b_qkv = grad_b_qkv[0].reshape(3, local_heads, head_dim)
        grad_w_out = grad_w_out.reshape(local_heads, head_dim, width)
        return (y_out, grad_x, sums[4], sums[5], grad_w_qkv, grad_b_qkv, grad_w_out, sums[3],
                sums[1], sums[2], grad_w_up, grad_b_up[0], grad_w_down, sums[0])

    return jax.shard_map(device_step, mesh=mesh, in_specs=in_specs, out_specs=out_specs, check_vma=False)
```

time: 301 us -> 256 us (0.85)
  Pallas kernels: 273 us -> 234 us
  other arithmetic: 4.48 us -> 0 us
    pallas_call x1 -> x0, Pallas kernels: 95.4 us -> none  [forward_call(): pl.pallas_call(functools.partial(forward_kernel, (chunk, local_heads, hea...]
    pallas_call x3 -> x4, Pallas kernels: 178 us -> 234 us  [single_call(): pl.pallas_call(kernel, out_shape=outs, in_specs=[ANY_SPEC if i in in_any...]
    another operation x7 -> x8, local copies, waits for them, and re-layouts: 1.3 us -> 5.46 us  [device_step(): jnp.stack([b_out, ln2_gain, ln2_bias, b_down, ln1_gain, ln1_bias, b_up, b...]
    broadcast_in_dim x3 -> x0, local copies, waits for them, and re-layouts: 3.83 us -> none  [the longest x1 1.29 us: device_step(): bu_own = jnp.broadcast_to(b_up[None], (8,) + b_up.shape)]
    unnamed x34 -> x20, local copies, waits for them, and re-layouts: 10.1 us -> 10.1 us
where the time goes in v1:
time: 256 us
  Pallas kernels  234 us (91%)
  local copies, waits for them, and re-layouts  21.1 us (8%)
    pallas_call x4, Pallas kernels, single_call(): pl.pallas_call(kernel, out_shape=outs, in_specs=[ANY_SPEC if i in in_any...  234 us
    unnamed x20, local copies, waits for them, and re-layouts  10.1 us
    another operation x8, local copies, waits for them, and re-layouts, device_step(): jnp.stack([b_out, ln2_gain, ln2_bias, b_down, ln1_gain, ln1_bias, b_up, b...  5.46 us

profile of v1, /device:TPU:0, one launch (start us, length us, event | category | flops | bytes accessed | tf_op | source)
XLA Modules:
  0.0 255.5 jit_solution(12425655118248019363)
XLA Ops:
  0.6 0.7 stack.29
  1.3 0.7 stack.30
  2.0 0.7 stack.25
  2.7 0.7 stack.26
  3.4 0.7 stack.27
  4.1 0.7 stack.31
  4.8 0.7 stack.28
  5.5 0.6 stack.32.vec_ref
  6.1 0.7 copy.32
  6.8 0.1 broadcast_in_dim.14
  6.9 0.6 broadcast_in_dim.15.bq_ref
  7.5 76.3 %forward.1 = (bf16[1024,640]{1,0:T(8,128)(2,1)}, bf16[4,480,640]{2,1,0:T(8,128)(2,1)}, bf16[1024,640]{1,0:T(8,128)(2,1)}, bf16[20,48,1024]{2,1,0:T(8,128)(2,1)},...) custom-call(bf16[4,256,640]{2,1,0:T(8,128)(2,1)} %x_ref.1, ...), custom_call_target="tpu_custom_call" | custom-call | tf_op jit(solution)/shard_map/forward/pallas_call | solution.py:530
  83.8 39.7 %middle.1 = (bf16[1024,640]{1,0:T(8,128)(2,1)}, bf16[1024,640]{1,0:T(8,128)(2,1)}, f32[640,1024]{1,0:T(8,128)}, bf16[1024,640]{1,0:T(8,128)(2,1)}, bf16[640,1024...) custom-call(bf16[1024,640]{1,0:T(8,128)(2,1)} %get-tuple-element.52.x_ref.x_in, ...), custom_call_target="tpu_custom_call" | custom-call | tf_op jit(solution)/shard_map/middle/pallas_call | solution.py:530
  123.5 78.5 %backward.1 = (bf16[4,3,160,1024]{3,2,1,0:T(8,128)(2,1)}, f32[4,3,160,128]{3,2,1,0:T(8,128)}, f32[160,640]{1,0:T(8,128)}, f32[320,640]{1,0:T(8,128)}, bf16[3,512...) custom-call(bf16[20,48,1024]{2,1,0:T(8,128)(2,1)} %get-tuple-element.49.q_in, ...), custom_call_target="tpu_custom_call" | custom-call | tf_op jit(solution)/shard_map/backward/pallas_call | solution.py:530
  202.0 1.7 slice_reduce_fusion
  203.7 0.1 broadcast_in_dim.16
  203.8 0.6 broadcast_in_dim.17.gb_ref
  204.4 0.0 copy-start.2
  204.4 39.3 %tail.1 = (bf16[4,256,640]{2,1,0:T(8,128)(2,1)}, f32[480,640]{1,0:T(8,128)}, f32[8,480]{1,0:T(8,128)}, f32[8,640]{1,0:T(8,128)}, f32[640,640]{1,0:T(8,128)}, /*index=5*/f32[8,640]{1,0:T(8,128)}, f32[640,640]{1,0:T(8,128)}) custom-call(bf16[4,480,1024]{2,1,0:T(8,128)(2,1)} %bitcast.14, f32[4,8,480]{2,1,0:T(8,128)} %broadcast_in_dim.17.gb_ref, ...), custom_call_target="tpu_custom_call" | custom-call | tf_op jit(solution)/shard_map/tail/pallas_call | solution.py:530
  243.7 0.7 slice_reduce_fusion.8
  244.5 0.1 reshape_squeeze.4
  244.5 0.6 copy.33
  245.2 1.6 slice_reduce_fusion.1
  246.8 0.0 copy-done.2
  246.8 0.0 copy-start.3
  246.8 1.1 copy.40
  247.8 0.7 copy-done.3
  248.6 0.0 copy-start.4
  248.6 1.1 copy.41
  249.6 0.7 copy-done.4
  250.3 0.0 copy-start.5
  250.3 0.0 copy-start.1
  250.3 1.0 copy.42
  251.4 0.2 copy-done.5
  251.6 0.8 copy.43
  252.3 0.0 copy-done.1
  252.3 0.0 copy-start
  252.3 1.2 copy.44
  253.5 0.9 copy-done
  254.4 1.2 copy.45
Async XLA Ops:
  204.4 42.4 %copy-start.2 = (bf16[4,256,640]{2,1,0:T(8,128)(2,1)S(1)}, bf16[4,256,640]{2,1,0:T(8,128)(2,1)}, u32[]{:S(2)}) copy-start(bf16[4,256,640]{2,1,0:T(8,128)(2,1)} %get-tuple-element.133) | copy-start | bytes 3932164
  246.8 1.8 copy-start.3
  248.6 1.8 copy-start.4
  250.3 1.3 copy-start.5
  250.3 2.0 copy-start.1
  252.3 2.0 copy-start
